TPU v7x, 128 devices: a whole 4x4x4 slice. The times are simulated.
128 devices in a mesh: rep: 32 (over x, y_hi, z), tp: 4 (over y_lo, core).
Axes of the slice: x: 4, y: 4 (y_hi: 2, y_lo: 2; y = y_hi * 2 + y_lo), z: 4, core: 2. Of those that a mesh axis runs over, the one named last changes fastest.
Arguments:
- q_weight: float32 [5120, 5120], P(('rep', 'tp')), may hold values from -0.078125 to 0.078125
- key_projection_weight: float32 [1024, 5120], P(('rep', 'tp')), may hold values from -0.078125 to 0.078125
- value_projection_weight: float32 [1024, 5120], P(('rep', 'tp')), may hold values from -0.078125 to 0.078125
- tokens: bfloat16 [32768, 5120], P(('rep', 'tp')), may hold values from -6 to 6
Outputs:
- combined_query_key_value: bfloat16 [7168, 5120], P('tp')
- projected: bfloat16 [32768, 7168], P('rep', 'tp')
All inputs are finite; a program needn't handle non-finite values.
Results may differ from a plain program's by a relative error of at most 0.0049.
Values may be sent and summed in bfloat16 or wider, within the bound.
A program may use at most 192 MiB of HBM per device.

v0:
```python
import jax
import jax.numpy as jnp
from jax import lax
from jax.sharding import Mesh
from jax.sharding import PartitionSpec as P

TP = ("tp_0", "tp_1")
REP_TP = ("rep", "tp_0", "tp_1")


def in_order(tiles, dim):
    dims = list(tiles.shape[1:])
    dims[dim] *= tiles.shape[0]
    return jnp.moveaxis(tiles, 0, dim).reshape(dims)


def stacked_from(x, axes, order):
    tiles = x
    for k in order:
        tiles = lax.all_gather(tiles, axes[k])
    done = order[::-1]
    back = [done.index(k) for k in range(len(axes))]
    tiles = tiles.transpose(*back, *range(len(axes), tiles.ndim))
    return tiles.reshape(-1, *x.shape)


def gathered_by_axis(x, axes, order, dim):
    return in_order(stacked_from(x, axes, order), dim)


def join_blocks(blocks, q_rows, key_value_rows):
    row_width = blocks.shape[3]
    bounds = ((0, q_rows), (q_rows, key_value_rows), (q_rows + key_value_rows, key_value_rows))
    pieces = []
    for row_start, length in bounds:
        part_rows = blocks[:, :, row_start : row_start + length]
        pieces.append(jnp.transpose(part_rows, (1, 0, 2, 3)).reshape(-1, row_width))
    return jnp.concatenate(pieces, 0)


def shards(q_weight, key_projection_weight, value_projection_weight, tokens):
    rep_size = lax.axis_size("rep")
    tp_size = lax.axis_size(TP)
    per_rank = rep_size // tp_size
    q_rows = q_weight.shape[0]
    key_value_rows = key_projection_weight.shape[0]
    width = q_weight.shape[1]
    shard_rows = jnp.concatenate(
        [q_weight, key_projection_weight, value_projection_weight], 0
    ).astype(jnp.bfloat16)
    row_count = shard_rows.shape[0]
    prompts = gathered_by_axis(tokens, TP, (0, 1), 0)
    col_width = width // rep_size
    split_cols = shard_rows.reshape(row_count, rep_size, col_width)
    arrived = lax.all_to_all(
        lax.all_to_all(split_cols, "rep", split_axis=1, concat_axis=1, tiled=True),
        TP,
        split_axis=1,
        concat_axis=1,
        tiled=True,
    )
    arranged = jnp.transpose(arrived.reshape(row_count, tp_size, per_rank, col_width), (1, 2, 0, 3))
    column_block = join_blocks(arranged, q_rows, key_value_rows)
    segment = lax.all_gather(column_block, "rep", axis=1, tiled=True)
    partial_sum = lax.dot_general(
        prompts, segment, (((1,), (1,)), ((), ())), preferred_element_type=jnp.float32
    )
    return (segment, partial_sum.astype(jnp.bfloat16))


def solution(mesh):
    split = Mesh(mesh.devices.reshape(mesh.shape["rep"], 2, 2), ("rep", "tp_0", "tp_1"))
    in_specs = (P(REP_TP, None), P(REP_TP, None), P(REP_TP, None), P(REP_TP, None))
    out_specs = (P(TP, None), P("rep", TP))
    return jax.shard_map(
        shards, mesh=split, in_specs=in_specs, out_specs=out_specs, check_vma=False
    )
```

profile of v0, /device:TPU:8, one launch (start us, length us, event | category | flops | bytes accessed | tf_op | source)
XLA Modules:
  0.0 352.8 jit_solution(4590002078311635463)
XLA Ops:
  7.2 0.0 copy-start.1
  7.2 0.0 copy-start.2
  7.2 0.0 copy-start
  7.2 0.0 all-gather.8.cloned.1.call-start
  7.2 0.7 all-gather.8.cloned.1.call-update
  7.9 0.0 all-gather.10.cloned.1.call-start
  8.0 73.9 %all-gather.8.cloned.1.call-done = bf16[512,5120]{1,0:T(8,128)(2,1)} async-done(((bf16[256,5120]{1,0:T(8,128)(2,1)}), bf16[512,5120]{1,0:T(8,128)(2,1)}) %all-gather.8.cloned.1.call-update) | async-done | bytes 5242896 | tf_op jit(solution)/shard_map/all_gather | solution.py:20
  81.9 0.0 all-gather.10.cloned.1.call-update
  81.9 0.0 all-gather.6.cloned.1.call-start
  82.0 0.0 copy-done.1
  82.0 0.2 concatenate.15
  82.2 0.0 copy-done.2
  82.2 0.2 concatenate.16
  82.4 0.0 copy-done
  82.4 0.8 concatenate.14
  83.3 0.2 pad_maximum_fusion
  83.5 0.5 copy.21
  84.0 25.6 %all_to_all.10 = bf16[56,32,160]{2,0,1:T(8,128)(2,1)S(1)} all-to-all(bf16[56,32,160]{2,0,1:T(8,128)(2,1)S(1)} %copy.21), channel_id=1, replica_groups=mesh['rep'=32,'tp_0'=2,'tp_1'=2] {'rep'}, dimensions={1} | all-to-all | bytes 1146880 | tf_op jit(solution)/shard_map/all_to_all | solution.py:56
  109.5 15.6 %all_to_all.11 = bf16[56,32,160]{2,0,1:T(8,128)(2,1)S(1)} all-to-all(bf16[56,32,160]{2,0,1:T(8,128)(2,1)S(1)} %all_to_all.10), channel_id=1, replica_groups=mesh['rep'=32,'tp_0'=2,'tp_1'=2] {'tp_0','tp_1'}, dimensions={1} | all-to-all | bytes 1146880 | tf_op jit(solution)/shard_map/all_to_all | solution.py:55
  125.1 0.2 copy.31
  125.4 0.4 copy.23
  125.8 0.1 copy.24
  125.9 0.1 copy.25
  126.0 0.2 pad_maximum_fusion.1
  126.1 1.1 copy.26
  127.2 0.0 all-gather.6.cloned.1.call-update
  127.2 0.0 all-gather.10.cloned.1.call-done
  127.3 8.8 %copy.27 = bf16[2,2,256,5120]{3,2,1,0:T(8,128)(2,1)} copy(bf16[2,2,256,5120]{3,2,0,1:T(8,128)(2,1)} %bitcast.23) | data formatting | bytes 20971520 | tf_op jit(solution)/shard_map/transpose | solution.py:23
  136.1 151.9 %all-gather.6.cloned.1.call-done = bf16[1792,5120]{0,1:T(8,128)(2,1)} async-done(((bf16[1792,160]{0,1:T(8,128)(2,1)}), bf16[1792,5120]{0,1:T(8,128)(2,1)}) %all-gather.6.cloned.1.call-update) | async-done | bytes 18350096 | tf_op jit(solution)/shard_map/all_gather | solution.py:64
  288.0 27.3 %fusion = bf16[1024,1792]{0,1:T(8,128)(2,1)} fusion(bf16[1792,5120]{0,1:T(8,128)(2,1)} %all-gather.6.cloned.1.call-done, bf16[1024,5120]{1,0:T(8,128)(2,1)} %bitcast.24), kind=kOutput, calls=%fused_computation.1 | convolution fusion | flops 18792316928 | bytes 32505856 | tf_op jit(solution)/shard_map/dot_general | solution.py:65
  315.3 5.9 %copy.29 = bf16[1024,1792]{1,0:T(8,128)(2,1)} copy(bf16[1024,1792]{0,1:T(8,128)(2,1)} %fusion) | data formatting | bytes 7340032
  321.2 25.1 %copy.28 = bf16[1792,5120]{1,0:T(8,128)(2,1)} copy(bf16[1792,5120]{0,1:T(8,128)(2,1)} %all-gather.6.cloned.1.call-done) | data formatting | bytes 36700160
  (5 shorter events, 0.1 us)
Async XLA Ops:
  7.2 74.8 %copy-start.1 = (f32[8,5120]{1,0:T(8,128)S(1)}, f32[8,5120]{1,0:T(8,128)}, u32[]{:S(2)}) copy-start(f32[8,5120]{1,0:T(8,128)} %param.5) | copy-start | bytes 491524
  7.2 75.0 %copy-start.2 = (f32[8,5120]{1,0:T(8,128)S(1)}, f32[8,5120]{1,0:T(8,128)}, u32[]{:S(2)}) copy-start(f32[8,5120]{1,0:T(8,128)} %param.6) | copy-start | bytes 491524
  7.2 75.2 %copy-start = (f32[40,5120]{1,0:T(8,128)S(1)}, f32[40,5120]{1,0:T(8,128)}, u32[]{:S(2)}) copy-start(f32[40,5120]{1,0:T(8,128)} %param.4) | copy-start | bytes 2457604
  7.2 74.7 %all-gather.8.cloned.1.call-start = ((), (), s32[]{:S(2)}) async-start(), calls=%async_computation.3 | async-start | bytes 7864320 | tf_op jit(solution)/shard_map/all_gather | solution.py:20
  7.9 119.3 %all-gather.10.cloned.1.call-start = ((), (), s32[]{:S(2)}) async-start(), calls=%async_computation.4 | async-start | bytes 15728640 | tf_op jit(solution)/shard_map/all_gather | solution.py:20
  81.9 206.1 %all-gather.6.cloned.1.call-start = ((), (), s32[]{:S(2)}) async-start(), calls=%async_computation.2 | async-start | bytes 18923520 | tf_op jit(solution)/shard_map/all_gather | solution.py:64
Sparse Core Ops, SparseCore 0:
  9.6 72.1 all-gather.7
  83.5 27.5 all-gather.9
  127.4 160.5 all-gather.5
where the time goes:
time: 355 us; the launch traced here: 353 us
  waiting for transfers between devices  227 us (64%)
  local copies, waits for them, and re-layouts  43.3 us (12%)
  blocking collectives  41.2 us (12%)
  matrix products  27.3 us (8%)
  between operations  13.9 us (4%)
    all_gather x1, waiting for transfers between devices, shards(): segment = lax.all_gather(column_block, 'rep', axis=1, tiled=True)  152 us
    all_gather x2, waiting for transfers between devices, stacked_from(): tiles = lax.all_gather(tiles, axes[k])  73.9 us
    unnamed x8, local copies, waits for them, and re-layouts  31 us
    dot_general x1, matrix products, shards(): lax.dot_general(prompts, segment, (((1,), (1,)), ((), ())), preferred_ele...  27.3 us
    all_to_all x1, blocking collectives, shards(): lax.all_to_all(split_cols, 'rep', split_axis=1, concat_axis=1, tiled=True)  25.6 us
    all_to_all x1, blocking collectives, shards(): lax.all_to_all(lax.all_to_all(split_cols, 'rep', split_axis=1, concat_axi...  15.6 us
    transpose x1, local copies, waits for them, and re-layouts, stacked_from(): tiles = tiles.transpose(*back, *range(len(axes), tiles.ndim))  8.78 us
  transfers between devices with their start and end apart: 3, of which 2 were waited for; matrix products, arithmetic and copies ran while one was open for 4% of the time, Pallas kernels for 0%

commit v1 on v0

v1 whole, which is shorter than its diff:
```python
import functools

import jax
import jax.numpy as jnp
from jax import lax
from jax.experimental import pallas as pl
from jax.experimental.pallas import tpu as pltpu
from jax.sharding import PartitionSpec as P

MESH = pl.DeviceIdType.MESH
SUB = 8


def gather_kernel(shape, shard, toks, w, t4, wsend, wrecv, psend, tsend, trecv, loc):
    qr, kr = shape
    n = qr + 2 * kr
    qn, kn = 32 * qr, 32 * kr
    rep, tp = lax.axis_index("rep"), lax.axis_index("tp")
    x, yh, z = rep // 8, (rep // 4) % 2, rep % 4
    thi, tlo = tp // 2, tp % 2

    def at(x_, yh_, z_):
        return x_ * 8 + yh_ * 4 + z_

    x1 = x + 1 - 2 * (x % 2)
    x3 = 3 - x
    role0 = x == tp
    role3 = x == 3 - tp

    def pieces(j):
        return tuple(
            pl.ds(pl.multiple_of(a + j * r, SUB), r)
            for a, r in ((0, qr), (qn, kr), (qn + kn, kr))
        )

    shard_pieces = (pl.ds(0, qr), pl.ds(qr, kr), pl.ds(qr + kr, kr))

    def whole(sem):
        return pltpu.make_async_copy(w.at[pl.ds(0, n)], w.at[pl.ds(0, n)], sem)

    def send(src, pairs, dst_sem, src_sem, dev):
        for s, d in pairs:
            pltpu.make_async_remote_copy(
                src_ref=src.at[s], dst_ref=w.at[d], send_sem=src_sem, recv_sem=dst_sem,
                device_id=dev, device_id_type=MESH,
            ).start()

    me = (yh * 4 + z) * 4 + tp
    pairs = list(zip(shard_pieces, pieces(me)))

    @pl.when(role0)
    def _():
        for s, d in pairs:
            pltpu.make_async_copy(shard.at[s], w.at[d], wrecv.at[me]).start()

    @pl.when(jnp.logical_not(role0))
    def _():
        send(shard, pairs, wrecv.at[me], psend.at[0], (rep, x))

    send(shard, pairs, wrecv.at[me], psend.at[1], (at(x, 1 - yh, z), x))

    rows = toks.shape[0]
    half = rows // 2

    def slot_rows(slot, part):
        return pl.ds(pl.multiple_of(slot * rows + part * half, half), half)

    sib = thi * 2 + (1 - tlo)
    far = (1 - thi) * 2 + tlo
    fars = (1 - thi) * 2 + (1 - tlo)
    own = pltpu.make_async_copy(toks, t4.at[pl.ds(pl.multiple_of(tp * rows, rows), rows)], loc)
    own.start()

    def tok(src, slot, part, sem, dev):
        return pltpu.make_async_remote_copy(
            src_ref=src, dst_ref=t4.at[slot_rows(slot, part)],
            send_sem=tsend.at[sem], recv_sem=trecv.at[slot, part],
            device_id=(rep, dev), device_id_type=MESH,
        )

    for part in range(2):
        tok(toks.at[pl.ds(part * half, half)], tp, part, part, far).start()
    for part in range(2):
        tok(toks.at[pl.ds(part * half, half)], tp, part, 2 + part, sib).start()

    def wait_tok(slot, part):
        ref = t4.at[slot_rows(slot, part)]
        pltpu.make_async_copy(ref, ref, trecv.at[slot, part]).wait()

    def relay(part):
        wait_tok(far, part)
        tok(t4.at[slot_rows(far, part)], far, part, 4 + part, sib).start()

    def plan(i, d):
        zs = (z + d) % 4
        h, m, c = i // 4, (i // 2) % 2, i % 2
        tq = ((thi + m + h) % 2) * 2 + (tlo + c) % 2
        j = (((yh + h) % 2) * 4 + zs) * 4 + tq
        odd = jnp.logical_and(c == 1, jnp.logical_or(i < 7, zs % 2 == 1))
        zact = jnp.logical_or(role0, jnp.logical_not(odd))
        xact = odd if d else jnp.bool_(True)
        out = []
        if d in (0, 3):
            c0 = zact if d == 0 else jnp.logical_and(zact, m == 0)
            out.append((0, c0, (at(x, yh, (z + 1) % 4), tp)))
        if d in (0, 1):
            c0 = zact if d == 0 else jnp.logical_and(zact, m == 1)
            out.append((1, c0, (at(x, yh, (z + 3) % 4), tp)))
        out.append((2, jnp.logical_and(jnp.logical_or(role0, role3), xact), (at(x1, yh, z), tp)))
        out.append((3, jnp.logical_and(role0, xact), (at(x3, yh, z), tp)))
        return j, out

    LAG = ((0, 0), (1, 1), (3, 1), (2, 2))

    def step(u, carry):
        for d, lag in LAG:
            i = u - lag

            @pl.when(jnp.logical_and(i >= 0, i < 8))
            def _(i=i, d=d):
                j, out = plan(i, d)
                whole(wrecv.at[j]).wait()
                for s, cond, dev in out:
                    @pl.when(cond)
                    def _(s=s, dev=dev):
                        pr = [(p, p) for p in pieces(j)]
                        send(w, pr, wrecv.at[j], wsend.at[s, i * 4 + d], dev)

        for part, when in ((0, 5), (1, 8)):
            @pl.when(u == when)
            def _(part=part):
                relay(part)
        return carry

    lax.fori_loop(0, 10, step, 0)

    own.wait()
    for slot in (sib, fars):
        for part in range(2):
            wait_tok(slot, part)
    for s in range(6):
        ref = t4.at[pl.ds(0, half)]
        pltpu.make_async_copy(ref, ref, tsend.at[s]).wait()

    @pl.when(jnp.logical_not(role0))
    def _():
        whole(psend.at[0]).wait()

    whole(psend.at[1]).wait()

    def drain(i, carry):
        for d in range(4):
            _, out = plan(i, d)
            for s, cond, _dev in out:
                @pl.when(cond)
                def _(s=s):
                    whole(wsend.at[s, i * 4 + d]).wait()
        return carry

    lax.fori_loop(0, 8, drain, 0)


def product_kernel(w, t, w_out, p_out, acc, wsem, psem):
    keep = pltpu.make_async_copy(w, w_out, wsem)
    keep.start()
    cols = 256

    def step(i, carry):
        at = pl.ds(pl.multiple_of(i * cols, cols), cols)
        acc[:, at] = lax.dot_general(
            t[...], w[at, :], (((1,), (1,)), ((), ())), preferred_element_type=jnp.float32
        ).astype(jnp.bfloat16)
        return carry

    lax.fori_loop(0, w.shape[0] // cols, step, 0)
    done = pltpu.make_async_copy(acc, p_out, psem)
    done.start()
    done.wait()
    keep.wait()


def shards(q_weight, key_projection_weight, value_projection_weight, tokens):
    width = q_weight.shape[1]
    qr, kr = q_weight.shape[0], key_projection_weight.shape[0]
    rows = 32 * (qr + 2 * kr)
    count = 4 * tokens.shape[0]
    shard = jnp.concatenate(
        [q_weight, key_projection_weight, value_projection_weight], 0
    ).astype(jnp.bfloat16)
    w, t = pl.pallas_call(
        functools.partial(gather_kernel, (qr, kr)),
        out_shape=(
            pltpu.VMEM((rows, width), jnp.bfloat16),
            pltpu.VMEM((count, width), jnp.bfloat16),
        ),
        in_specs=[
            pl.BlockSpec(memory_space=pltpu.VMEM),
            pl.BlockSpec(memory_space=pl.ANY),
        ],
        out_specs=(pl.BlockSpec(memory_space=pl.ANY),) * 2,
        scratch_shapes=[
            pltpu.SemaphoreType.DMA((4, 32)),
            pltpu.SemaphoreType.DMA((32,)),
            pltpu.SemaphoreType.DMA((2,)),
            pltpu.SemaphoreType.DMA((6,)),
            pltpu.SemaphoreType.DMA((4, 2)),
            pltpu.SemaphoreType.DMA,
        ],
        compiler_params=pltpu.CompilerParams(
            has_side_effects=True, vmem_limit_bytes=4 << 20
        ),
        name="gather",
    )(shard, pltpu.with_memory_space_constraint(tokens, pltpu.HBM))
    return pl.pallas_call(
        product_kernel,
        out_shape=(
            jax.ShapeDtypeStruct((rows, width), jnp.bfloat16),
            jax.ShapeDtypeStruct((count, rows), jnp.bfloat16),
        ),
        in_specs=[pl.BlockSpec(memory_space=pltpu.VMEM)] * 2,
        out_specs=(pl.BlockSpec(memory_space=pltpu.HBM),) * 2,
        scratch_shapes=[
            pltpu.VMEM((count, rows), jnp.bfloat16),
            pltpu.SemaphoreType.DMA,
            pltpu.SemaphoreType.DMA,
        ],
        compiler_params=pltpu.CompilerParams(vmem_limit_bytes=20 << 20),
        name="product",
    )(
        pltpu.with_memory_space_constraint(w, pltpu.VMEM),
        pltpu.with_memory_space_constraint(t, pltpu.VMEM),
    )


def solution(mesh):
    both = P(("rep", "tp"), None)
    return jax.shard_map(
        shards, mesh=mesh, in_specs=(both,) * 4, out_specs=(P("tp", None), P("rep", "tp")),
        check_vma=False,
    )
```

time: 355 us -> 201 us (0.57)
  waiting for transfers between devices: 227 us -> 0 us
  Pallas kernels: 0 us -> 183 us
  blocking collectives: 41.2 us -> 0 us
  local copies, waits for them, and re-layouts: 43.3 us -> 12.9 us
  matrix products: 27.3 us -> 0 us
  between operations: 13.9 us -> 0.66 us
    all_gather x3 -> x0, waiting for transfers between devices: 226 us -> none  [the longest x1 152 us: shards(): segment = lax.all_gather(column_block, 'rep', axis=1, tiled=True)]
    pallas_call x0 -> x2, Pallas kernels: none -> 183 us  [the longest x1 161 us: shards(): pl.pallas_call(functools.partial(gather_kernel, (qr, kr)), out_shape=(plt...]
    all_to_all x2 -> x0, blocking collectives: 41.2 us -> none  [the longest x1 25.6 us: shards(): lax.all_to_all(split_cols, 'rep', split_axis=1, concat_axis=1, tiled=True)]
    dot_general x1 -> x0, matrix products: 27.3 us -> none  [shards(): lax.dot_general(prompts, segment, (((1,), (1,)), ((), ())), preferred_ele...]
    unnamed x8 -> x4, local copies, waits for them, and re-layouts: 31 us -> 12.9 us
    transpose x6 -> x0, local copies, waits for them, and re-layouts: 9.37 us -> none  [the longest x1 8.78 us: stacked_from(): tiles = tiles.transpose(*back, *range(len(axes), tiles.ndim))]
  transfers between devices with their start and end apart: 3 -> 0, of which waited for: 2 -> 0; matrix products, arithmetic and copies ran while one was open for 4% -> 0% of each run, Pallas kernels for 0% -> 0%
where the time goes in v1:
time: 201 us; the launch traced here: 200 us
  Pallas kernels  183 us (91%)
  local copies, waits for them, and re-layouts  12.9 us (6%)
  other arithmetic  3.08 us (2%)
    pallas_call x1, Pallas kernels, shards(): pl.pallas_call(functools.partial(gather_kernel, (qr, kr)), out_shape=(plt...  161 us
    pallas_call x1, Pallas kernels, shards(): pl.pallas_call(product_kernel, out_shape=(jax.ShapeDtypeStruct((rows, wid...  22.2 us
    unnamed x4, local copies, waits for them, and re-layouts  12.9 us

profile of v1, /device:TPU:8, one launch (start us, length us, event | category | flops | bytes accessed | tf_op | source)
XLA Modules:
  0.0 199.6 jit_solution(11589432237053969963)
XLA Ops:
  0.6 0.9 convert.10
  1.6 0.9 convert.11
  2.5 1.2 convert.9
  3.7 160.8 %gather.1 = (bf16[1792,5120]{1,0:T(8,128)(2,1)S(1)}, bf16[1024,5120]{1,0:T(8,128)(2,1)S(1)}) custom-call(bf16[56,5120]{1,0:T(8,128)(2,1)S(1)} %pad_maximum_fusion.shard, bf16[256,5120]{1,0:T(8,128)(2,1)} %toks.1), custom_call_target="tpu_custom_call" | custom-call | tf_op jit(solution)/shard_map/gather/pallas_call | solution.py:190
  164.6 0.0 copy-start
  164.6 6.7 %copy-done = bf16[1792,5120]{1,0:T(8,128)(2,1)} copy-done((bf16[1792,5120]{1,0:T(8,128)(2,1)}, bf16[1792,5120]{1,0:T(8,128)(2,1)S(1)}, u32[]{:S(2)}) %copy-start) | copy-done | bytes 18350104
  171.3 0.0 copy-start.1
  171.3 6.2 %copy-done.1 = bf16[1792,5120]{1,0:T(8,128)(2,1)S(1)} copy-done((bf16[1792,5120]{1,0:T(8,128)(2,1)S(1)}, bf16[1792,5120]{1,0:T(8,128)(2,1)}, u32[]{:S(2)}) %copy-start.1) | copy-done | bytes 18350104
  177.5 22.2 %product.1 = (bf16[1792,5120]{1,0:T(8,128)(2,1)}, bf16[1024,1792]{1,0:T(8,128)(2,1)}) custom-call(bf16[1792,5120]{1,0:T(8,128)(2,1)S(1)} %copy-done.1, bf16[1024,5120]{1,0:T(8,128)(2,1)S(1)} %get-tuple-element.5.t), custom_call_target="tpu_custom_call" | custom-call | tf_op jit(solution)/shard_map/product/pallas_call | solution.py:214
  (1 shorter events, 0.0 us)
Async XLA Ops:
  164.6 6.7 %copy-start = (bf16[1792,5120]{1,0:T(8,128)(2,1)}, bf16[1792,5120]{1,0:T(8,128)(2,1)S(1)}, u32[]{:S(2)}) copy-start(bf16[1792,5120]{1,0:T(8,128)(2,1)S(1)} %get-tuple-element.4.w) | copy-start | bytes 55050244
  171.3 6.2 %copy-start.1 = (bf16[1792,5120]{1,0:T(8,128)(2,1)S(1)}, bf16[1792,5120]{1,0:T(8,128)(2,1)}, u32[]{:S(2)}) copy-start(bf16[1792,5120]{1,0:T(8,128)(2,1)} %copy-done) | copy-start | bytes 55050244

commit v2 on v0

v2 whole, which is shorter than its diff:
```python
import functools

import jax
import jax.numpy as jnp
from jax import lax
from jax.experimental import pallas as pl
from jax.experimental.pallas import tpu as pltpu
from jax.sharding import PartitionSpec as P

MESH = pl.DeviceIdType.MESH
SUB = 8
COLS = 128

CLASSES = "BCBABBBc"
HALF = (0, 0, 1, 1, 0, 0, 1, 1)
ORDER = (
    (0, 0), (1, 0), (2, 0), (3, 0), (0, 1), (1, 1), (0, 3), (1, 3),
    (4, 0), (2, 1), (3, 3), (3, 1), (5, 0), (2, 3), (1, 2), (0, 2),
    (3, 2), (2, 2), (7, 0), (6, 0), (4, 1), (4, 3), (5, 3), (7, 3),
    (6, 1), (7, 2), (5, 1), (6, 3), (4, 2), (7, 1), (5, 2), (6, 2),
)
MULTIPLY_AT = 24
RELAY_AT = (13, 19)


def early_blocks(yh):
    return ((yh * 5, yh * 5 + 1), (yh * 5 + 2, yh * 5 + 3), (10 + yh, 12 + yh))


def late_blocks(yh):
    o = 1 - yh
    return (
        (yh * 5 + 4, o * 5), (o * 5 + 1, o * 5 + 2), (o * 5 + 3, o * 5 + 4), (10 + o, 12 + o),
    )


def block(b):
    return pl.ds(pl.multiple_of(b * COLS, COLS), COLS)


def pair_product(t, w, rows, pair):
    both = jnp.concatenate([w[block(pair[0]), :], w[block(pair[1]), :]], 0)
    return lax.dot_general(
        t[rows, :], both, (((1,), (1,)), ((), ())), preferred_element_type=jnp.float32
    ).astype(jnp.bfloat16)


def gather_kernel(shape, shard, toks, w, t4, acc, wsend, wrecv, psend, tsend, trecv, loc):
    qr, kr = shape
    n = qr + 2 * kr
    qn, kn = 32 * qr, 32 * kr
    cut = qr // SUB // 2 * SUB + SUB
    rep, tp = lax.axis_index("rep"), lax.axis_index("tp")
    x, yh, z = rep // 8, (rep // 4) % 2, rep % 4
    thi, tlo = tp // 2, tp % 2

    def at(x_, yh_, z_):
        return x_ * 8 + yh_ * 4 + z_

    x1 = x + 1 - 2 * (x % 2)
    x3 = 3 - x
    role0 = x == tp
    role3 = x == 3 - tp
    flip = at(x, 1 - yh, z)
    zp, zm = at(x, yh, (z + 1) % 4), at(x, yh, (z + 3) % 4)
    px1, px3 = at(x1, yh, z), at(x3, yh, z)

    barrier = pltpu.get_barrier_semaphore()
    peers = [(rep, (tp + k) % 4) for k in (1, 2, 3)]
    peers += [(flip, (tp + k) % 4) for k in range(4)]
    peers += [(p, tp) for p in (zp, zm, px1, px3)]
    for peer in peers:
        pl.semaphore_signal(barrier, inc=1, device_id=peer, device_id_type=MESH)
    pl.semaphore_wait(barrier, len(peers))

    def spans(j, part):
        if part == 0:
            return ((j * qr, cut),)
        return ((j * qr + cut, qr - cut), (qn + j * kr, kr), (qn + kn + j * kr, kr))

    def own_spans(part):
        if part == 0:
            return ((0, cut),)
        return ((cut, qr - cut), (qr, kr), (qr + kr, kr))

    def cut_of(ref, span):
        return ref.at[pl.ds(pl.multiple_of(span[0], SUB), span[1])]

    def settle(part, sem):
        size = cut if part == 0 else n - cut
        pltpu.make_async_copy(w.at[pl.ds(0, size)], w.at[pl.ds(0, size)], sem).wait()

    def send(src, src_spans, j, part, src_sem, dev):
        for s, d in zip(src_spans, spans(j, part)):
            pltpu.make_async_remote_copy(
                src_ref=cut_of(src, s), dst_ref=cut_of(w, d), send_sem=src_sem,
                recv_sem=wrecv.at[j * 2 + part], device_id=dev, device_id_type=MESH,
            ).start()

    me = (yh * 4 + z) * 4 + tp
    for part in range(2):
        @pl.when(role0)
        def _(part=part):
            for s, d in zip(own_spans(part), spans(me, part)):
                pltpu.make_async_copy(cut_of(shard, s), cut_of(w, d), wrecv.at[me * 2 + part]).start()

        @pl.when(jnp.logical_not(role0))
        def _(part=part):
            send(shard, own_spans(part), me, part, psend.at[0, part], (rep, x))

    crosses = jnp.logical_and(thi == x // 2, tlo != x % 2)
    for part in range(2):
        @pl.when(jnp.logical_not(crosses))
        def _(part=part):
            send(shard, own_spans(part), me, part, psend.at[1, part], (flip, x))

    rows = toks.shape[0]
    pieces = len(RELAY_AT)
    size = rows // pieces
    sib = thi * 2 + (1 - tlo)
    far = (1 - thi) * 2 + tlo
    fars = (1 - thi) * 2 + (1 - tlo)
    own = pltpu.make_async_copy(toks, t4.at[pl.ds(pl.multiple_of(tp * rows, rows), rows)], loc)
    own.start()

    def slot(r, part):
        return t4.at[pl.ds(pl.multiple_of(r * rows + part * size, size), size)]

    def tok(src, r, part, sem, dev):
        return pltpu.make_async_remote_copy(
            src_ref=src, dst_ref=slot(r, part), send_sem=tsend.at[sem, part],
            recv_sem=trecv.at[r, part], device_id=(rep, dev), device_id_type=MESH,
        )

    for kind, dev in ((0, far), (1, sib)):
        for part in range(pieces):
            tok(toks.at[pl.ds(part * size, size)], tp, part, kind, dev).start()

    def token_wait(r, part):
        pltpu.make_async_copy(slot(r, part), slot(r, part), trecv.at[r, part]).wait()

    def shard_of(i, d):
        h, m, c = i // 4, (i // 2) % 2, i % 2
        zs = (z + d) % 4
        tq = ((thi + m + h) % 2) * 2 + (tlo + c) % 2
        return (((yh + h) % 2) * 4 + zs) * 4 + tq

    def sends_of(i, d):
        kind = CLASSES[i]
        upward = (HALF[i] + tlo) % 2 == 0
        out = []
        if kind != "c":
            only = None if kind == "B" else role0
            if d in (0, 3):
                out.append((zp, only if d == 0 else upward if only is None else jnp.logical_and(only, upward)))
            if d in (0, 1):
                down = jnp.logical_not(upward)
                out.append((zm, only if d == 0 else down if only is None else jnp.logical_and(only, down)))
        if kind == "C":
            out.append((flip, role0))
        if kind != "B" or d == 0:
            out.append((px1, jnp.logical_or(role0, role3)))
            out.append((px3, role0))
        return out

    def guarded(cond, fn):
        if cond is None:
            fn()
        else:
            pl.when(cond)(fn)

    issued = []

    def multiply(piece):
        pair = early_blocks(yh)[piece // 2]
        half = t4.shape[0] // 2
        at_rows = pl.ds(piece % 2 * half, half)
        got = pair_product(t4, w, at_rows, pair)
        for k in range(2):
            acc[at_rows, block(pair[k])] = got[:, k * COLS : (k + 1) * COLS]

    for step, (i, d) in enumerate(ORDER):
        if step == MULTIPLY_AT:
            own.wait()
            for r in (sib, fars):
                for part in range(pieces):
                    token_wait(r, part)
        if MULTIPLY_AT <= step < MULTIPLY_AT + 6:
            multiply(step - MULTIPLY_AT)
        j = shard_of(i, d)
        for part in range(2):
            settle(part, wrecv.at[j * 2 + part])
            for dev, cond in sends_of(i, d):
                sem = wsend.at[len(issued)]
                guarded(cond, lambda dev=dev, sem=sem, part=part: send(w, spans(j, part), j, part, sem, (dev, tp)))
                issued.append((part, cond, sem))
        for part, when in enumerate(RELAY_AT):
            if step == when:
                token_wait(far, part)
                tok(slot(far, part), far, part, 2, sib).start()

    for kind in range(3):
        for part in range(pieces):
            pltpu.make_async_copy(slot(0, 0), slot(0, 0), tsend.at[kind, part]).wait()
    for part in range(2):
        guarded(jnp.logical_not(role0), lambda part=part: settle(part, psend.at[0, part]))
        guarded(jnp.logical_not(crosses), lambda part=part: settle(part, psend.at[1, part]))
    for part, cond, sem in issued:
        guarded(cond, lambda part=part, sem=sem: settle(part, sem))


def send_count():
    count = 0
    for kind in CLASSES:
        count += {"B": 4 + 2 + 2 * 0, "A": 4 + 2 + 6, "C": 4 + 2 + 6 + 4, "c": 8}[kind]
    return 2 * count


def product_kernel(w, t, acc, w_out, p_out, rest, wsem, psem):
    keep = pltpu.make_async_copy(w, w_out, wsem)
    keep.start()
    yh = (lax.axis_index("rep") // 4) % 2
    puts = []

    def put(src, b):
        puts.append(pltpu.make_async_copy(src, p_out.at[:, block(b)], psem.at[len(puts)]))
        puts[-1].start()

    for pair in early_blocks(yh):
        for b in pair:
            put(acc.at[:, block(b)], b)
    for k, pair in enumerate(late_blocks(yh)):
        rest[k] = pair_product(t, w, slice(None), pair)
        for m in range(2):
            put(rest.at[k, :, pl.ds(m * COLS, COLS)], pair[m])
    for p in puts:
        p.wait()
    keep.wait()


def shards(q_weight, key_projection_weight, value_projection_weight, tokens):
    width = q_weight.shape[1]
    qr, kr = q_weight.shape[0], key_projection_weight.shape[0]
    rows = 32 * (qr + 2 * kr)
    count = 4 * tokens.shape[0]
    shard = jnp.concatenate(
        [q_weight, key_projection_weight, value_projection_weight], 0
    ).astype(jnp.bfloat16)
    inside = [
        pltpu.VMEM((rows, width), jnp.bfloat16),
        pltpu.VMEM((count, width), jnp.bfloat16),
        pltpu.VMEM((count, rows), jnp.bfloat16),
    ]
    held = pl.pallas_call(
        functools.partial(gather_kernel, (qr, kr)),
        out_shape=inside,
        in_specs=[
            pl.BlockSpec(memory_space=pltpu.VMEM),
            pl.BlockSpec(memory_space=pl.ANY),
        ],
        out_specs=[pl.BlockSpec(memory_space=pltpu.VMEM)] * 3,
        scratch_shapes=[
            pltpu.SemaphoreType.DMA((send_count(),)),
            pltpu.SemaphoreType.DMA((64,)),
            pltpu.SemaphoreType.DMA((2, 2)),
            pltpu.SemaphoreType.DMA((3, len(RELAY_AT))),
            pltpu.SemaphoreType.DMA((4, len(RELAY_AT))),
            pltpu.SemaphoreType.DMA,
        ],
        compiler_params=pltpu.CompilerParams(
            has_side_effects=True, collective_id=0, vmem_limit_bytes=12 << 20
        ),
        name="gather",
    )(shard, pltpu.with_memory_space_constraint(tokens, pltpu.HBM))
    return pl.pallas_call(
        product_kernel,
        out_shape=(
            jax.ShapeDtypeStruct((rows, width), jnp.bfloat16),
            jax.ShapeDtypeStruct((count, rows), jnp.bfloat16),
        ),
        in_specs=[pl.BlockSpec(memory_space=pltpu.VMEM)] * 3,
        out_specs=(pl.BlockSpec(memory_space=pltpu.HBM),) * 2,
        scratch_shapes=[
            pltpu.VMEM((4, count, 2 * COLS), jnp.bfloat16),
            pltpu.SemaphoreType.DMA,
            pltpu.SemaphoreType.DMA((14,)),
        ],
        compiler_params=pltpu.CompilerParams(vmem_limit_bytes=8 << 20),
        name="product",
    )(*(pltpu.with_memory_space_constraint(a, pltpu.VMEM) for a in held))


def solution(mesh):
    both = P(("rep", "tp"), None)
    return jax.shard_map(
        shards, mesh=mesh, in_specs=(both,) * 4, out_specs=(P("tp", None), P("rep", "tp")),
        check_vma=False,
    )
```

time: 355 us -> 160 us (0.45)
  waiting for transfers between devices: 227 us -> 0 us
  Pallas kernels: 0 us -> 156 us
  local copies, waits for them, and re-layouts: 43.3 us -> 0 us
  blocking collectives: 41.2 us -> 0 us
  matrix products: 27.3 us -> 0 us
  between operations: 13.9 us -> 0.82 us
    all_gather x3 -> x0, waiting for transfers between devices: 226 us -> none  [the longest x1 152 us: shards(): segment = lax.all_gather(column_block, 'rep', axis=1, tiled=True)]
    pallas_call x0 -> x2, Pallas kernels: none -> 156 us  [the longest x1 143 us: shards(): pl.pallas_call(functools.partial(gather_kernel, (qr, kr)), out_shape=insi...]
    all_to_all x2 -> x0, blocking collectives: 41.2 us -> none  [the longest x1 25.6 us: shards(): lax.all_to_all(split_cols, 'rep', split_axis=1, concat_axis=1, tiled=True)]
    unnamed x8 -> x0, local copies, waits for them, and re-layouts: 31 us -> none
    dot_general x1 -> x0, matrix products: 27.3 us -> none  [shards(): lax.dot_general(prompts, segment, (((1,), (1,)), ((), ())), preferred_ele...]
    transpose x6 -> x0, local copies, waits for them, and re-layouts: 9.37 us -> none  [the longest x1 8.78 us: stacked_from(): tiles = tiles.transpose(*back, *range(len(axes), tiles.ndim))]
  transfers between devices with their start and end apart: 3 -> 0, of which waited for: 2 -> 0; matrix products, arithmetic and copies ran while one was open for 4% -> 0% of each run, Pallas kernels for 0% -> 0%
where the time goes in v2:
time: 160 us
  Pallas kernels  156 us (98%)
  other arithmetic  3.08 us (2%)
    pallas_call x1, Pallas kernels, shards(): pl.pallas_call(functools.partial(gather_kernel, (qr, kr)), out_shape=insi...  143 us
    pallas_call x1, Pallas kernels, shards(): pl.pallas_call(product_kernel, out_shape=(jax.ShapeDtypeStruct((rows, wid...  13.2 us

profile of v2, /device:TPU:8, one launch (start us, length us, event | category | flops | bytes accessed | tf_op | source)
XLA Modules:
  0.0 160.0 jit_solution(361727789554750476)
XLA Ops:
  0.6 0.9 convert.10
  1.6 0.9 convert.11
  2.5 1.2 convert.9
  3.7 142.9 %gather.1 = (bf16[1792,5120]{1,0:T(8,128)(2,1)S(1)}, bf16[1024,5120]{1,0:T(8,128)(2,1)S(1)}, bf16[1024,1792]{1,0:T(8,128)(2,1)S(1)}) custom-call(bf16[56,5120]{1,0:T(8,128)(2,1)S(1)} %pad_maximum_fusion.shard, bf16[256,5120]{1,0:T(8,128)(2,1)} %toks.1), custom_call_target="tpu_custom_call" | custom-call | tf_op jit(solution)/shard_map/gather/pallas_call | solution.py:254
  146.6 13.2 %product.1 = (bf16[1792,5120]{1,0:T(8,128)(2,1)}, bf16[1024,1792]{1,0:T(8,128)(2,1)}) custom-call(bf16[1792,5120]{1,0:T(8,128)(2,1)S(1)} %get-tuple-element.5.w, bf16[1024,5120]{1,0:T(8,128)(2,1)S(1)} %get-tuple-element.6.t, bf16[1024,1792]{1,0:T(8,128)(2,1)S(1)} %get-tuple-element.7.acc), custom_call_target="tpu_custom_call" | custom-call | tf_op jit(solution)/shard_map/product/pallas_call | solution.py:275
  (1 shorter events, 0.0 us)

commit v3 on v2

--- a/solution.py
+++ b/solution.py
@@ -11,27 +11,40 @@
 SUB = 8
 COLS = 128
 
-CLASSES = "BCBABBBc"
-HALF = (0, 0, 1, 1, 0, 0, 1, 1)
+CLASSES = "BCBMBBBc"
+HALF = (1, 0, 1, 1, 0, 0, 0, 0)
 ORDER = (
-    (0, 0), (1, 0), (2, 0), (3, 0), (0, 1), (1, 1), (0, 3), (1, 3),
-    (4, 0), (2, 1), (3, 3), (3, 1), (5, 0), (2, 3), (1, 2), (0, 2),
-    (3, 2), (2, 2), (7, 0), (6, 0), (4, 1), (4, 3), (5, 3), (7, 3),
-    (6, 1), (7, 2), (5, 1), (6, 3), (4, 2), (7, 1), (5, 2), (6, 2),
+    (
+        0, 4, 12, 1, 16, 13, 8, 15, 20, 24, 7, 5, 9, 23, 3, 28,
+        14, 11, 31, 6, 25, 29, 21, 30, 10, 27, 2, 17, 19, 22, 26, 18,
+    ),
+    (
+        0, 16, 13, 8, 12, 15, 1, 9, 20, 3, 11, 14, 24, 28, 4, 7,
+        10, 17, 23, 2, 6, 21, 5, 31, 25, 27, 29, 19, 22, 26, 30, 18,
+    ),
+    (
+        0, 3, 4, 16, 8, 9, 15, 13, 20, 7, 1, 5, 24, 21, 12, 17,
+        23, 19, 11, 14, 2, 27, 25, 28, 6, 31, 10, 18, 29, 26, 22, 30,
+    ),
+    (
+        0, 3, 4, 1, 12, 16, 15, 13, 8, 20, 7, 24, 5, 23, 14, 28,
+        2, 19, 31, 9, 17, 11, 25, 6, 29, 27, 10, 21, 18, 30, 22, 26,
+    ),
 )
-MULTIPLY_AT = 24
-RELAY_AT = (13, 19)
+MULTIPLY_AT = 27
+RELAY_AT = (11, 23)
+PIECES = 12
+MULTIPLY_PARTS = (0, 1)
 
 
 def early_blocks(yh):
     return ((yh * 5, yh * 5 + 1), (yh * 5 + 2, yh * 5 + 3), (10 + yh, 12 + yh))
 
 
-def late_blocks(yh):
+def late_blocks(yh, k):
     o = 1 - yh
-    return (
-        (yh * 5 + 4, o * 5), (o * 5 + 1, o * 5 + 2), (o * 5 + 3, o * 5 + 4), (10 + o, 12 + o),
-    )
+    first = jnp.where(k == 0, yh * 5 + 4, jnp.where(k == 3, 10 + o, o * 5 + 2 * k - 1))
+    return first, jnp.where(k == 3, 12 + o, o * 5 + 2 * k)
 
 
 def block(b):
@@ -60,7 +73,6 @@
     x1 = x + 1 - 2 * (x % 2)
     x3 = 3 - x
     role0 = x == tp
-    role3 = x == 3 - tp
     flip = at(x, 1 - yh, z)
     zp, zm = at(x, yh, (z + 1) % 4), at(x, yh, (z + 3) % 4)
     px1, px3 = at(x1, yh, z), at(x3, yh, z)
@@ -145,22 +157,21 @@
         tq = ((thi + m + h) % 2) * 2 + (tlo + c) % 2
         return (((yh + h) % 2) * 4 + zs) * 4 + tq
 
-    def sends_of(i, d):
+    def sends_of(role, i, d):
         kind = CLASSES[i]
         upward = (HALF[i] + tlo) % 2 == 0
         out = []
-        if kind != "c":
-            only = None if kind == "B" else role0
+        if kind == "B" or (role == 0 and kind in "AMC") or (role == 3 and kind == "M"):
             if d in (0, 3):
-                out.append((zp, only if d == 0 else upward if only is None else jnp.logical_and(only, upward)))
+                out.append((zp, None if d == 0 else upward))
             if d in (0, 1):
-                down = jnp.logical_not(upward)
-                out.append((zm, only if d == 0 else down if only is None else jnp.logical_and(only, down)))
-        if kind == "C":
-            out.append((flip, role0))
-        if kind != "B" or d == 0:
-            out.append((px1, jnp.logical_or(role0, role3)))
-            out.append((px3, role0))
+                out.append((zm, None if d == 0 else jnp.logical_not(upward)))
+        if kind == "C" and role == 0:
+            out.append((flip, None))
+        if role in (0, 3) and (kind != "B" or d == 0):
+            out.append((px1, None))
+        if role == 0 and (kind in "ACc" or d == 0):
+            out.append((px3, None))
         return out
 
     def guarded(cond, fn):
@@ -169,35 +180,45 @@
         else:
             pl.when(cond)(fn)
 
-    issued = []
+    role = (x % 2 + tlo) % 2 + 2 * ((x // 2 + thi) % 2)
+    issued = [[], [], [], []]
+    lines = t4.shape[0] // (PIECES // 3)
 
     def multiply(piece):
-        pair = early_blocks(yh)[piece // 2]
-        half = t4.shape[0] // 2
-        at_rows = pl.ds(piece % 2 * half, half)
+        pair = early_blocks(yh)[piece % 3]
+        at_rows = pl.ds(piece // 3 * lines, lines)
         got = pair_product(t4, w, at_rows, pair)
         for k in range(2):
             acc[at_rows, block(pair[k])] = got[:, k * COLS : (k + 1) * COLS]
 
-    for step, (i, d) in enumerate(ORDER):
+    def forward(k, step, part):
+        i, d = divmod(ORDER[k][step], 4)
+        j = shard_of(i, d)
+        settle(part, wrecv.at[j * 2 + part])
+        for n, (dev, cond) in enumerate(sends_of(k, i, d)):
+            sem = wsend.at[len(issued[k])]
+            guarded(cond, lambda dev=dev, sem=sem: send(w, spans(j, part), j, part, sem, (dev, tp)))
+            issued[k].append((part, i, d, n))
+
+    done = 0
+    for step in range(32):
         if step == MULTIPLY_AT:
             own.wait()
             for r in (sib, fars):
                 for part in range(pieces):
                     token_wait(r, part)
-        if MULTIPLY_AT <= step < MULTIPLY_AT + 6:
-            multiply(step - MULTIPLY_AT)
-        j = shard_of(i, d)
         for part in range(2):
-            settle(part, wrecv.at[j * 2 + part])
-            for dev, cond in sends_of(i, d):
-                sem = wsend.at[len(issued)]
-                guarded(cond, lambda dev=dev, sem=sem, part=part: send(w, spans(j, part), j, part, sem, (dev, tp)))
-                issued.append((part, cond, sem))
+            if step >= MULTIPLY_AT and done < PIECES and part in MULTIPLY_PARTS:
+                multiply(done)
+                done += 1
+            for k in range(4):
+                pl.when(role == k)(lambda k=k, part=part: forward(k, step, part))
         for part, when in enumerate(RELAY_AT):
             if step == when:
                 token_wait(far, part)
                 tok(slot(far, part), far, part, 2, sib).start()
+    for piece in range(done, PIECES):
+        multiply(piece)
 
     for kind in range(3):
         for part in range(pieces):
@@ -205,37 +226,61 @@
     for part in range(2):
         guarded(jnp.logical_not(role0), lambda part=part: settle(part, psend.at[0, part]))
         guarded(jnp.logical_not(crosses), lambda part=part: settle(part, psend.at[1, part]))
-    for part, cond, sem in issued:
-        guarded(cond, lambda part=part, sem=sem: settle(part, sem))
+
+    def drain(k):
+        for at_sem, (part, i, d, n) in enumerate(issued[k]):
+            cond = sends_of(k, i, d)[n][1]
+            guarded(cond, lambda at_sem=at_sem, part=part: settle(part, wsend.at[at_sem]))
+
+    for k in range(4):
+        pl.when(role == k)(lambda k=k: drain(k))
 
 
 def send_count():
-    count = 0
-    for kind in CLASSES:
-        count += {"B": 4 + 2 + 2 * 0, "A": 4 + 2 + 6, "C": 4 + 2 + 6 + 4, "c": 8}[kind]
-    return 2 * count
+    return 2 * sum({"B": 6, "A": 12, "M": 9, "C": 16, "c": 8}[kind] for kind in CLASSES)
 
 
 def product_kernel(w, t, acc, w_out, p_out, rest, wsem, psem):
     keep = pltpu.make_async_copy(w, w_out, wsem)
     keep.start()
     yh = (lax.axis_index("rep") // 4) % 2
-    puts = []
-
-    def put(src, b):
-        puts.append(pltpu.make_async_copy(src, p_out.at[:, block(b)], psem.at[len(puts)]))
-        puts[-1].start()
-
-    for pair in early_blocks(yh):
-        for b in pair:
-            put(acc.at[:, block(b)], b)
-    for k, pair in enumerate(late_blocks(yh)):
-        rest[k] = pair_product(t, w, slice(None), pair)
-        for m in range(2):
-            put(rest.at[k, :, pl.ds(m * COLS, COLS)], pair[m])
-    for p in puts:
+
+    def put(src, b, sem):
+        return pltpu.make_async_copy(src, p_out.at[:, block(b)], sem)
+
+    early = [b for pair in early_blocks(yh) for b in pair]
+    early = [put(acc.at[:, block(b)], b, psem.at[8 + n]) for n, b in enumerate(early)]
+    for p in early:
+        p.start()
+
+    def late(k):
+        pair = late_blocks(yh, k)
+        return [put(rest.at[k, :, pl.ds(m * COLS, COLS)], pair[m], psem.at[2 * k + m]) for m in range(2)]
+
+    def step(k, carry):
+        rest[k] = pair_product(t, w, slice(None), late_blocks(yh, k))
+        for p in late(k):
+            p.start()
+        return carry
+
+    lax.fori_loop(0, 4, step, 0)
+
+    def finish(k, carry):
+        for p in late(k):
+            p.wait()
+        return carry
+
+    lax.fori_loop(0, 4, finish, 0)
+    for p in early:
         p.wait()
     keep.wait()
+
+
+def cast_kernel(q, k, v, out):
+    at = 0
+    for part in (q, k, v):
+        out[pl.ds(at, part.shape[0]), :] = part[...].astype(jnp.bfloat16)
+        at += part.shape[0]
 
 
 def shards(q_weight, key_projection_weight, value_projection_weight, tokens):
@@ -243,9 +288,14 @@
     qr, kr = q_weight.shape[0], key_projection_weight.shape[0]
     rows = 32 * (qr + 2 * kr)
     count = 4 * tokens.shape[0]
-    shard = jnp.concatenate(
-        [q_weight, key_projection_weight, value_projection_weight], 0
-    ).astype(jnp.bfloat16)
+    shard = pl.pallas_call(
+        cast_kernel,
+        out_shape=pltpu.VMEM((qr + 2 * kr, width), jnp.bfloat16),
+        in_specs=[pl.BlockSpec(memory_space=pltpu.VMEM)] * 3,
+        out_specs=pl.BlockSpec(memory_space=pltpu.VMEM),
+        compiler_params=pltpu.CompilerParams(vmem_limit_bytes=4 << 20),
+        name="cast",
+    )(q_weight, key_projection_weight, value_projection_weight)
     inside = [
         pltpu.VMEM((rows, width), jnp.bfloat16),
         pltpu.VMEM((count, width), jnp.bfloat16),
@@ -271,7 +321,10 @@
             has_side_effects=True, collective_id=0, vmem_limit_bytes=12 << 20
         ),
         name="gather",
-    )(shard, pltpu.with_memory_space_constraint(tokens, pltpu.HBM))
+    )(
+        pltpu.with_memory_space_constraint(shard, pltpu.VMEM),
+        pltpu.with_memory_space_constraint(tokens, pltpu.HBM),
+    )
     return pl.pallas_call(
         product_kernel,
         out_shape=(

time: 160 us -> 150 us (0.938)
  Pallas kernels: 156 us -> 146 us
  other arithmetic: 3.08 us -> 0 us
  local copies, waits for them, and re-layouts: 0 us -> 2.97 us
    pallas_call x1, Pallas kernels: 143 us -> 133 us  [shards(): pl.pallas_call(functools.partial(gather_kernel, (qr, kr)), out_shape=insi...]
    another operation x3 -> x0, other arithmetic: 3.04 us -> none
    unnamed x0 -> x6, local copies, waits for them, and re-layouts: none -> 2.97 us
where the time goes in v3:
time: 150 us; the launch traced here: 149 us
  Pallas kernels  146 us (97%)
  local copies, waits for them, and re-layouts  2.97 us (2%)
    pallas_call x1, Pallas kernels, shards(): pl.pallas_call(functools.partial(gather_kernel, (qr, kr)), out_shape=insi...  133 us
    pallas_call x1, Pallas kernels, shards(): pl.pallas_call(product_kernel, out_shape=(jax.ShapeDtypeStruct((rows, wid...  12.6 us

profile of v3, /device:TPU:8, one launch (start us, length us, event | category | flops | bytes accessed | tf_op | source)
XLA Modules:
  0.0 149.4 jit_solution(15912350703508735744)
XLA Ops:
  0.6 0.0 copy-start
  0.6 1.1 copy-done
  1.8 0.0 copy-start.1
  1.8 0.9 copy-done.1
  2.7 0.0 copy-start.2
  2.7 0.9 copy-done.2
  3.6 0.1 cast.1.shard
  3.7 133.0 %gather.1 = (bf16[1792,5120]{1,0:T(8,128)(2,1)S(1)}, bf16[1024,5120]{1,0:T(8,128)(2,1)S(1)}, bf16[1024,1792]{1,0:T(8,128)(2,1)S(1)}) custom-call(bf16[56,5120]{1,0:T(8,128)(2,1)S(1)} %cast.1.shard, bf16[256,5120]{1,0:T(8,128)(2,1)} %toks.1), custom_call_target="tpu_custom_call" | custom-call | tf_op jit(solution)/shard_map/gather/pallas_call | solution.py:304
  136.6 12.6 %product.1 = (bf16[1792,5120]{1,0:T(8,128)(2,1)}, bf16[1024,1792]{1,0:T(8,128)(2,1)}) custom-call(bf16[1792,5120]{1,0:T(8,128)(2,1)S(1)} %get-tuple-element.5.w, bf16[1024,5120]{1,0:T(8,128)(2,1)S(1)} %get-tuple-element.6.t, bf16[1024,1792]{1,0:T(8,128)(2,1)S(1)} %get-tuple-element.7.acc), custom_call_target="tpu_custom_call" | custom-call | tf_op jit(solution)/shard_map/product/pallas_call | solution.py:328
Async XLA Ops:
  0.6 1.1 copy-start
  1.8 0.9 copy-start.1
  2.7 0.9 copy-start.2

commit v4 on v3

--- a/solution.py
+++ b/solution.py
@@ -11,30 +11,33 @@
 SUB = 8
 COLS = 128
 
-CLASSES = "BCBMBBBc"
-HALF = (1, 0, 1, 1, 0, 0, 0, 0)
+CLASSES = ("MBMMMBBA", "MCBBBBBc")
+TREES = ("qkqqwqww", "qqkwkqqq")
+HALF = ((0, 1, 0, 1, 1, 0, 1, 1), (0, 1, 0, 1, 0, 1, 0, 0))
 ORDER = (
     (
-        0, 4, 12, 1, 16, 13, 8, 15, 20, 24, 7, 5, 9, 23, 3, 28,
-        14, 11, 31, 6, 25, 29, 21, 30, 10, 27, 2, 17, 19, 22, 26, 18,
+        0, 1, 6, 8, 24, 9, 25, 30, 7, 14, 16, 17, 15, 10, 2, 11, 3, 18, 5, 33, 26, 40,
+        4, 22, 56, 32, 23, 48, 20, 27, 49, 13, 35, 12, 46, 58, 62, 19, 41, 39, 50, 42, 34, 31,
+        29, 21, 59, 28, 38, 63, 47, 51, 36, 43, 55, 57, 60, 61, 54, 37, 44, 53, 45, 52,
     ),
     (
-        0, 16, 13, 8, 12, 15, 1, 9, 20, 3, 11, 14, 24, 28, 4, 7,
-        10, 17, 23, 2, 6, 21, 5, 31, 25, 27, 29, 19, 22, 26, 30, 18,
+        0, 8, 5, 3, 25, 31, 30, 4, 56, 40, 6, 16, 26, 9, 27, 24, 15, 14, 17, 20, 42, 11,
+        13, 22, 7, 2, 29, 1, 48, 10, 49, 19, 46, 62, 18, 23, 41, 58, 38, 54, 44, 32, 34, 33,
+        50, 28, 21, 12, 51, 35, 55, 57, 47, 39, 36, 60, 43, 59, 63, 52, 53, 61, 37, 45,
     ),
     (
-        0, 3, 4, 16, 8, 9, 15, 13, 20, 7, 1, 5, 24, 21, 12, 17,
-        23, 19, 11, 14, 2, 27, 25, 28, 6, 31, 10, 18, 29, 26, 22, 30,
+        0, 1, 6, 3, 8, 17, 25, 9, 56, 22, 26, 31, 15, 11, 27, 14, 23, 18, 10, 30, 40, 13,
+        19, 2, 29, 12, 48, 32, 4, 7, 16, 33, 21, 42, 24, 54, 28, 46, 50, 20, 49, 41, 62, 5,
+        35, 38, 39, 34, 52, 55, 51, 36, 58, 43, 47, 63, 57, 37, 59, 44, 60, 53, 61, 45,
     ),
     (
-        0, 3, 4, 1, 12, 16, 15, 13, 8, 20, 7, 24, 5, 23, 14, 28,
-        2, 19, 31, 9, 17, 11, 25, 6, 29, 27, 10, 21, 18, 30, 22, 26,
+        0, 2, 8, 24, 1, 3, 7, 6, 30, 17, 15, 4, 16, 23, 22, 18, 10, 25, 32, 14, 26, 5,
+        9, 48, 19, 31, 27, 11, 40, 13, 33, 56, 12, 46, 28, 21, 29, 50, 20, 34, 49, 38, 39, 42,
+        54, 44, 41, 62, 36, 58, 43, 55, 59, 51, 35, 63, 52, 57, 47, 61, 60, 53, 45, 37,
     ),
 )
-MULTIPLY_AT = 27
-RELAY_AT = (11, 23)
-PIECES = 12
-MULTIPLY_PARTS = (0, 1)
+MULTIPLY_AT = (48, 49, 49, 52, 55, 59)
+RELAY_AT = (31, 32)
 
 
 def early_blocks(yh):
@@ -120,9 +123,17 @@
         def _(part=part):
             send(shard, own_spans(part), me, part, psend.at[0, part], (rep, x))
 
-    crosses = jnp.logical_and(thi == x // 2, tlo != x % 2)
+    seen = 4 + 2 * (1 - (thi + x // 2) % 2) + (tlo + x) % 2
+
+    def goes_early(part):
+        keep = jnp.bool_(True)
+        for i in range(4, 8):
+            if CLASSES[part][i] == "c":
+                keep = jnp.logical_and(keep, seen != i)
+        return keep
+
     for part in range(2):
-        @pl.when(jnp.logical_not(crosses))
+        @pl.when(goes_early(part))
         def _(part=part):
             send(shard, own_spans(part), me, part, psend.at[1, part], (flip, x))
 
@@ -157,9 +168,9 @@
         tq = ((thi + m + h) % 2) * 2 + (tlo + c) % 2
         return (((yh + h) % 2) * 4 + zs) * 4 + tq
 
-    def sends_of(role, i, d):
-        kind = CLASSES[i]
-        upward = (HALF[i] + tlo) % 2 == 0
+    def sends_of(role, i, d, part):
+        kind, tree = CLASSES[part][i], TREES[part][i]
+        upward = (HALF[part][i] + tlo) % 2 == 0
         out = []
         if kind == "B" or (role == 0 and kind in "AMC") or (role == 3 and kind == "M"):
             if d in (0, 3):
@@ -168,9 +179,16 @@
                 out.append((zm, None if d == 0 else jnp.logical_not(upward)))
         if kind == "C" and role == 0:
             out.append((flip, None))
-        if role in (0, 3) and (kind != "B" or d == 0):
+        if kind == "M":
+            near, over = role in (0, 3), role == 0 and d == 0
+        elif kind == "B" and d != 0:
+            near, over = False, False
+        else:
+            near = role in {"q": (0, 3), "w": (0,), "k": (3,)}[tree]
+            over = role in {"q": (0,), "w": (0, 1), "k": (0, 2)}[tree]
+        if near:
             out.append((px1, None))
-        if role == 0 and (kind in "ACc" or d == 0):
+        if over:
             out.append((px3, None))
         return out
 
@@ -182,54 +200,52 @@
 
     role = (x % 2 + tlo) % 2 + 2 * ((x // 2 + thi) % 2)
     issued = [[], [], [], []]
-    lines = t4.shape[0] // (PIECES // 3)
+    lines = t4.shape[0] // (len(MULTIPLY_AT) // 3)
 
     def multiply(piece):
+        if piece == 0:
+            own.wait()
+            for r in (sib, fars):
+                for part in range(pieces):
+                    token_wait(r, part)
         pair = early_blocks(yh)[piece % 3]
         at_rows = pl.ds(piece // 3 * lines, lines)
         got = pair_product(t4, w, at_rows, pair)
         for k in range(2):
             acc[at_rows, block(pair[k])] = got[:, k * COLS : (k + 1) * COLS]
 
-    def forward(k, step, part):
-        i, d = divmod(ORDER[k][step], 4)
+    def forward(k, step):
+        i, d, part = ORDER[k][step] // 8, ORDER[k][step] // 2 % 4, ORDER[k][step] % 2
         j = shard_of(i, d)
         settle(part, wrecv.at[j * 2 + part])
-        for n, (dev, cond) in enumerate(sends_of(k, i, d)):
+        for n, (dev, cond) in enumerate(sends_of(k, i, d, part)):
             sem = wsend.at[len(issued[k])]
             guarded(cond, lambda dev=dev, sem=sem: send(w, spans(j, part), j, part, sem, (dev, tp)))
             issued[k].append((part, i, d, n))
 
-    done = 0
-    for step in range(32):
-        if step == MULTIPLY_AT:
-            own.wait()
-            for r in (sib, fars):
-                for part in range(pieces):
-                    token_wait(r, part)
-        for part in range(2):
-            if step >= MULTIPLY_AT and done < PIECES and part in MULTIPLY_PARTS:
-                multiply(done)
-                done += 1
-            for k in range(4):
-                pl.when(role == k)(lambda k=k, part=part: forward(k, step, part))
+    for step in range(65):
+        for piece, when in enumerate(MULTIPLY_AT):
+            if step == when:
+                multiply(piece)
+        if step == 64:
+            break
+        for k in range(4):
+            pl.when(role == k)(lambda k=k: forward(k, step))
         for part, when in enumerate(RELAY_AT):
             if step == when:
                 token_wait(far, part)
                 tok(slot(far, part), far, part, 2, sib).start()
-    for piece in range(done, PIECES):
-        multiply(piece)
 
     for kind in range(3):
         for part in range(pieces):
             pltpu.make_async_copy(slot(0, 0), slot(0, 0), tsend.at[kind, part]).wait()
     for part in range(2):
         guarded(jnp.logical_not(role0), lambda part=part: settle(part, psend.at[0, part]))
-        guarded(jnp.logical_not(crosses), lambda part=part: settle(part, psend.at[1, part]))
+        guarded(goes_early(part), lambda part=part: settle(part, psend.at[1, part]))
 
     def drain(k):
         for at_sem, (part, i, d, n) in enumerate(issued[k]):
-            cond = sends_of(k, i, d)[n][1]
+            cond = sends_of(k, i, d, part)[n][1]
             guarded(cond, lambda at_sem=at_sem, part=part: settle(part, wsend.at[at_sem]))
 
     for k in range(4):
@@ -237,7 +253,8 @@
 
 
 def send_count():
-    return 2 * sum({"B": 6, "A": 12, "M": 9, "C": 16, "c": 8}[kind] for kind in CLASSES)
+    most = {"B": 6, "A": 12, "M": 9, "C": 16, "c": 8}
+    return max(32, sum(most[kind] for line in CLASSES for kind in line))
 
 
 def product_kernel(w, t, acc, w_out, p_out, rest, wsem, psem):
@@ -276,11 +293,16 @@
     keep.wait()
 
 
-def cast_kernel(q, k, v, out):
-    at = 0
-    for part in (q, k, v):
-        out[pl.ds(at, part.shape[0]), :] = part[...].astype(jnp.bfloat16)
+def cast_kernel(q, k, v, out, wide, sems):
+    at, parts = 0, []
+    for n, part in enumerate((q, k, v)):
+        rows = pl.ds(at, part.shape[0])
+        parts.append((rows, pltpu.make_async_copy(part, wide.at[rows], sems.at[n])))
+        parts[-1][1].start()
         at += part.shape[0]
+    for rows, copy in parts:
+        copy.wait()
+        out[rows, :] = wide[rows, :].astype(jnp.bfloat16)
 
 
 def shards(q_weight, key_projection_weight, value_projection_weight, tokens):
@@ -291,11 +313,18 @@
     shard = pl.pallas_call(
         cast_kernel,
         out_shape=pltpu.VMEM((qr + 2 * kr, width), jnp.bfloat16),
-        in_specs=[pl.BlockSpec(memory_space=pltpu.VMEM)] * 3,
+        in_specs=[pl.BlockSpec(memory_space=pltpu.HBM)] * 3,
         out_specs=pl.BlockSpec(memory_space=pltpu.VMEM),
+        scratch_shapes=[
+            pltpu.VMEM((qr + 2 * kr, width), jnp.float32),
+            pltpu.SemaphoreType.DMA((3,)),
+        ],
         compiler_params=pltpu.CompilerParams(vmem_limit_bytes=4 << 20),
         name="cast",
-    )(q_weight, key_projection_weight, value_projection_weight)
+    )(*(
+        pltpu.with_memory_space_constraint(a, pltpu.HBM)
+        for a in (q_weight, key_projection_weight, value_projection_weight)
+    ))
     inside = [
         pltpu.VMEM((rows, width), jnp.bfloat16),
         pltpu.VMEM((count, width), jnp.bfloat16),

time: 150 us -> 142 us (0.947)
  Pallas kernels: 146 us -> 141 us
  local copies, waits for them, and re-layouts: 2.97 us -> 0 us
    pallas_call x1, Pallas kernels: 133 us -> 127 us  [shards(): pl.pallas_call(functools.partial(gather_kernel, (qr, kr)), out_shape=insi...]
    unnamed x6 -> x0, local copies, waits for them, and re-layouts: 2.97 us -> none
where the time goes in v4:
time: 142 us
  Pallas kernels  141 us (99%)
    pallas_call x1, Pallas kernels, shards(): pl.pallas_call(functools.partial(gather_kernel, (qr, kr)), out_shape=insi...  127 us
    pallas_call x1, Pallas kernels, shards(): pl.pallas_call(product_kernel, out_shape=(jax.ShapeDtypeStruct((rows, wid...  12.6 us

profile of v4, /device:TPU:8, one launch (start us, length us, event | category | flops | bytes accessed | tf_op | source)
XLA Modules:
  0.0 142.1 jit_solution(2625153236622883350)
XLA Ops:
  0.6 1.2 cast.1.shard
  1.9 127.4 %gather.1 = (bf16[1792,5120]{1,0:T(8,128)(2,1)S(1)}, bf16[1024,5120]{1,0:T(8,128)(2,1)S(1)}, bf16[1024,1792]{1,0:T(8,128)(2,1)S(1)}) custom-call(bf16[56,5120]{1,0:T(8,128)(2,1)S(1)} %cast.1.shard, bf16[256,5120]{1,0:T(8,128)(2,1)} %toks.1), custom_call_target="tpu_custom_call" | custom-call | tf_op jit(solution)/shard_map/gather/pallas_call | solution.py:333
  129.3 12.6 %product.1 = (bf16[1792,5120]{1,0:T(8,128)(2,1)}, bf16[1024,1792]{1,0:T(8,128)(2,1)}) custom-call(bf16[1792,5120]{1,0:T(8,128)(2,1)S(1)} %get-tuple-element.5.w, bf16[1024,5120]{1,0:T(8,128)(2,1)S(1)} %get-tuple-element.6.t, bf16[1024,1792]{1,0:T(8,128)(2,1)S(1)} %get-tuple-element.7.acc), custom_call_target="tpu_custom_call" | custom-call | tf_op jit(solution)/shard_map/product/pallas_call | solution.py:357

commit v5 on v4

--- a/solution.py
+++ b/solution.py
@@ -12,32 +12,32 @@
 COLS = 128
 
 CLASSES = ("MBMMMBBA", "MCBBBBBc")
-TREES = ("qkqqwqww", "qqkwkqqq")
-HALF = ((0, 1, 0, 1, 1, 0, 1, 1), (0, 1, 0, 1, 0, 1, 0, 0))
+TREES = ("kkwqwwww", "qqkwkqqq")
+HALF = ((1, 1, 0, 0, 1, 0, 1, 0), (0, 1, 0, 1, 0, 1, 1, 1))
 ORDER = (
     (
-        0, 1, 6, 8, 24, 9, 25, 30, 7, 14, 16, 17, 15, 10, 2, 11, 3, 18, 5, 33, 26, 40,
-        4, 22, 56, 32, 23, 48, 20, 27, 49, 13, 35, 12, 46, 58, 62, 19, 41, 39, 50, 42, 34, 31,
-        29, 21, 59, 28, 38, 63, 47, 51, 36, 43, 55, 57, 60, 61, 54, 37, 44, 53, 45, 52,
+        0, 1, 24, 2, 16, 9, 8, 17, 6, 7, 25, 23, 19, 3, 11, 14, 27, 40, 48, 32, 33, 10,
+        30, 22, 5, 26, 56, 18, 15, 4, 31, 13, 49, 20, 62, 12, 41, 34, 21, 28, 58, 35, 59, 39,
+        29, 51, 63, 55, 38, 50, 57, 42, 54, 60, 43, 53, 37, 61, 46, 47, 36, 44, 52, 45,
     ),
     (
-        0, 8, 5, 3, 25, 31, 30, 4, 56, 40, 6, 16, 26, 9, 27, 24, 15, 14, 17, 20, 42, 11,
-        13, 22, 7, 2, 29, 1, 48, 10, 49, 19, 46, 62, 18, 23, 41, 58, 38, 54, 44, 32, 34, 33,
-        50, 28, 21, 12, 51, 35, 55, 57, 47, 39, 36, 60, 43, 59, 63, 52, 53, 61, 37, 45,
+        2, 0, 40, 16, 46, 25, 7, 22, 6, 27, 1, 8, 42, 9, 31, 32, 24, 17, 56, 5, 18, 10,
+        4, 48, 30, 14, 13, 3, 15, 26, 49, 19, 23, 29, 20, 62, 41, 12, 21, 28, 51, 55, 33, 11,
+        54, 58, 50, 63, 34, 43, 47, 57, 39, 59, 35, 60, 44, 52, 38, 53, 61, 45, 37, 36,
     ),
     (
-        0, 1, 6, 3, 8, 17, 25, 9, 56, 22, 26, 31, 15, 11, 27, 14, 23, 18, 10, 30, 40, 13,
-        19, 2, 29, 12, 48, 32, 4, 7, 16, 33, 21, 42, 24, 54, 28, 46, 50, 20, 49, 41, 62, 5,
-        35, 38, 39, 34, 52, 55, 51, 36, 58, 43, 47, 63, 57, 37, 59, 44, 60, 53, 61, 45,
+        26, 1, 8, 30, 6, 16, 0, 17, 10, 19, 25, 23, 4, 27, 31, 2, 40, 11, 3, 14, 22, 9,
+        32, 33, 5, 12, 48, 18, 28, 7, 21, 24, 42, 49, 13, 29, 62, 34, 39, 20, 50, 54, 41, 15,
+        35, 55, 52, 56, 43, 51, 38, 46, 57, 47, 59, 44, 61, 45, 63, 58, 60, 36, 37, 53,
     ),
     (
-        0, 2, 8, 24, 1, 3, 7, 6, 30, 17, 15, 4, 16, 23, 22, 18, 10, 25, 32, 14, 26, 5,
-        9, 48, 19, 31, 27, 11, 40, 13, 33, 56, 12, 46, 28, 21, 29, 50, 20, 34, 49, 38, 39, 42,
-        54, 44, 41, 62, 36, 58, 43, 55, 59, 51, 35, 63, 52, 57, 47, 61, 60, 53, 45, 37,
+        0, 1, 16, 24, 6, 30, 26, 2, 8, 22, 17, 3, 25, 40, 4, 7, 19, 32, 33, 48, 14, 5,
+        11, 18, 31, 10, 28, 27, 46, 13, 54, 50, 23, 9, 21, 49, 12, 20, 29, 34, 38, 41, 47, 15,
+        59, 42, 56, 63, 35, 57, 52, 62, 55, 51, 43, 39, 58, 36, 61, 37, 60, 53, 45, 44,
     ),
 )
-MULTIPLY_AT = (48, 49, 49, 52, 55, 59)
-RELAY_AT = (31, 32)
+MULTIPLY_AT = (45, 46, 48, 48, 51, 55)
+RELAY_AT = (28, 34)
 
 
 def early_blocks(yh):

time: 142 us -> 138 us (0.972)
  Pallas kernels: 141 us -> 137 us
    pallas_call x1, Pallas kernels: 127 us -> 123 us  [shards(): pl.pallas_call(functools.partial(gather_kernel, (qr, kr)), out_shape=insi...]
where the time goes in v5:
time: 138 us
  Pallas kernels  137 us (99%)
    pallas_call x1, Pallas kernels, shards(): pl.pallas_call(functools.partial(gather_kernel, (qr, kr)), out_shape=insi...  123 us
    pallas_call x1, Pallas kernels, shards(): pl.pallas_call(product_kernel, out_shape=(jax.ShapeDtypeStruct((rows, wid...  12.6 us

profile of v5, /device:TPU:8, one launch (start us, length us, event | category | flops | bytes accessed | tf_op | source)
XLA Modules:
  0.0 138.1 jit_solution(10781592553394475431)
XLA Ops:
  0.6 1.2 cast.1.shard
  1.9 123.5 %gather.1 = (bf16[1792,5120]{1,0:T(8,128)(2,1)S(1)}, bf16[1024,5120]{1,0:T(8,128)(2,1)S(1)}, bf16[1024,1792]{1,0:T(8,128)(2,1)S(1)}) custom-call(bf16[56,5120]{1,0:T(8,128)(2,1)S(1)} %cast.1.shard, bf16[256,5120]{1,0:T(8,128)(2,1)} %toks.1), custom_call_target="tpu_custom_call" | custom-call | tf_op jit(solution)/shard_map/gather/pallas_call | solution.py:333
  125.4 12.6 %product.1 = (bf16[1792,5120]{1,0:T(8,128)(2,1)}, bf16[1024,1792]{1,0:T(8,128)(2,1)}) custom-call(bf16[1792,5120]{1,0:T(8,128)(2,1)S(1)} %get-tuple-element.5.w, bf16[1024,5120]{1,0:T(8,128)(2,1)S(1)} %get-tuple-element.6.t, bf16[1024,1792]{1,0:T(8,128)(2,1)S(1)} %get-tuple-element.7.acc), custom_call_target="tpu_custom_call" | custom-call | tf_op jit(solution)/shard_map/product/pallas_call | solution.py:357
